TPU v7x, 32 devices: a whole 2x2x4 slice. The times are simulated.
32 devices in a mesh: leaf: 8 (over z, y), grp: 4 (over x, core).
Axes of the slice: x: 2, y: 2, z: 4, core: 2. Of those that a mesh axis runs over, the one named last changes fastest.
Arguments:
- points: bfloat16 [32768, 256], P(('leaf', 'grp')), may hold values from -0.75 to 0.75
- rhs: float32 [32768, 128], P(('leaf', 'grp')), may hold values from -0.8 to 0.8
- permutation: int32 [32768], P(('leaf', 'grp')), may hold values from 0 to 32767, as said below
- leaf_basis: float32 [8192, 1024], P(('leaf', 'grp')), may hold values from -0.1875 to 0.1875
- climb_leaf: float32 [8192, 256], P(('leaf', 'grp')), may hold values from -0.25 to 0.25
- climb_pair: float32 [4096, 256], P(('leaf', 'grp')), may hold values from -0.25 to 0.25
- climb_quad: float32 [2048, 256], P(('leaf', 'grp')), may hold values from -0.25 to 0.25
- skel_points: bfloat16 [1024, 256], P(('leaf', 'grp')), may hold values from -0.75 to 0.75
- near_lists: int32 [32, 8], replicated, may hold values from -1 to 31, as said below
- far_lists: int32 [4, 3], replicated, may hold values from -1 to 3, as said below
Outputs:
- product: float32 [32768, 128], P(('leaf', 'grp'))
Inputs may be any that keep to these rules, and one draw needn't show every extreme that they name: `permutation`: maps each block of 1024 tree positions of one leaf onto the same block of initial indices, each once. `near_lists`: row t starts with t itself, then distinct other leaves of the same aligned block of eight (t // 8), then -1 entries only; some row has 8 leaves. `far_lists`: row m holds one or more distinct nodes other than m first, then -1 entries only; some row has 3 nodes.
All inputs are finite; a program needn't handle non-finite values.
Results may differ from a plain program's by a relative error of at most 0.0003.
Values may be sent and summed in bfloat16 or wider, within the bound.
No kernel may reach another device: no remote copies, remote signals or barrier semaphores. Data moves between devices by JAX's collectives and lax.ppermute only.
A program may use at most 128 MiB of HBM per device.

v0:
```python
import jax
import jax.numpy as jnp
from jax import lax
from jax.sharding import PartitionSpec as P


def partner(value, axis, distance):
    mask = 2**distance
    pairs = [(source, source ^ mask) for source in range(lax.axis_size(axis))]
    return lax.ppermute(value, axis, pairs)


def kernel_block(left, right):
    inner = jnp.dot(left, right.T, preferred_element_type=jnp.float32)
    left_sq = jnp.sum(jnp.square(left.astype(jnp.float32)), axis=1)
    right_sq = jnp.sum(jnp.square(right.astype(jnp.float32)), axis=1)
    product = left_sq[:, None] * right_sq[None, :]
    sine = jnp.sqrt(jnp.maximum(product - inner * inner, 0.0))
    theta = jnp.arctan2(sine, inner)
    return (sine + (jnp.pi - theta) * inner) / jnp.pi


def body(
    points,
    rhs,
    permutation,
    leaf_basis,
    climb_leaf,
    climb_pair,
    climb_quad,
    skel_points,
    near_lists,
    far_lists,
):
    upper_limit = lax.Precision.HIGHEST
    leaf_size = points.shape[0]
    rank = climb_leaf.shape[1]
    width = rhs.shape[1]
    local = permutation % leaf_size
    tree_pts = points[local]
    tree_weight = rhs[local]
    leaf_idx = lax.axis_index("leaf")
    grp_idx = lax.axis_index("grp")
    flat = leaf_idx * lax.axis_size("grp") + grp_idx
    position = flat % 8
    node = flat // 8
    parity = leaf_idx % 2
    skeleton_level_zero = jnp.dot(leaf_basis, tree_weight, precision=upper_limit)
    part_one = jnp.dot(climb_leaf.T, skeleton_level_zero, precision=upper_limit)
    skel_one = part_one + partner(part_one, "grp", 0)
    half = rank // 2
    rows_one = lax.dynamic_slice_in_dim(skel_one, flat % 2 * half, half, 0)
    part_two = jnp.dot(climb_pair.T, rows_one, precision=upper_limit)
    skel_two = lax.psum(part_two, "grp")
    quarter = rank // 4
    rows_two = lax.dynamic_slice_in_dim(skel_two, grp_idx * quarter, quarter, 0)
    part_three = jnp.dot(climb_quad.T, rows_two, precision=upper_limit)
    inner_sum = lax.psum(part_three, "grp")
    skel_three = inner_sum + partner(inner_sum, "leaf", 0)
    eighth = rank // 8
    weight_rows = lax.dynamic_slice_in_dim(skel_three, position * eighth, eighth, 0)
    all_pts = lax.all_gather(skel_points, ("leaf", "grp"), axis=0, tiled=True)
    all_weights = lax.all_gather(weight_rows, ("leaf", "grp"), axis=0, tiled=True)
    own_skel = lax.dynamic_slice_in_dim(all_pts, node * rank, rank, 0)
    far_kernel = kernel_block(own_skel, all_pts)
    col_node = jnp.arange(all_pts.shape[0]) // rank
    far_row = lax.dynamic_slice_in_dim(far_lists, node, 1, 0)[0]
    selected_rows = jnp.any(col_node[:, None] == far_row[None, :], axis=1).astype(jnp.float32)
    up_three = jnp.dot(far_kernel * selected_rows[None, :], all_weights, precision=upper_limit)
    up_two = lax.all_gather(
        jnp.dot(climb_quad, up_three, precision=upper_limit), "grp", axis=0, tiled=True
    )
    mine_half = jnp.dot(climb_pair, up_two, precision=upper_limit)
    other_half = partner(mine_half, "grp", 0)
    up_one = jnp.where(
        flat % 2 == 0,
        jnp.concatenate([mine_half, other_half], 0),
        jnp.concatenate([other_half, mine_half], 0),
    )
    upward_level_zero = jnp.dot(climb_leaf, up_one, precision=upper_limit)
    distant_field = jnp.dot(leaf_basis.T, upward_level_zero, precision=upper_limit)
    four_pts = lax.all_gather(tree_pts, "grp", axis=0, tiled=True)
    four_w = lax.all_gather(tree_weight, "grp", axis=0, tiled=True)
    other_pts = partner(four_pts, "leaf", 0)
    other_w = partner(four_w, "leaf", 0)
    group_pts = jnp.where(
        parity == 0,
        jnp.concatenate([four_pts, other_pts], 0),
        jnp.concatenate([other_pts, four_pts], 0),
    )
    group_w = jnp.where(
        parity == 0, jnp.concatenate([four_w, other_w], 0), jnp.concatenate([other_w, four_w], 0)
    )
    start_leaf = node * 8

    def nearby_block(target, source):
        left = lax.dynamic_slice_in_dim(group_pts, target * leaf_size, leaf_size, 0)
        right = lax.dynamic_slice_in_dim(group_pts, source * leaf_size, leaf_size, 0)
        source_w = lax.dynamic_slice_in_dim(group_w, source * leaf_size, leaf_size, 0)
        return jnp.dot(kernel_block(left, right), source_w, precision=upper_limit)

    group_rows = lax.dynamic_slice_in_dim(near_lists, start_leaf, 8, 0)
    columns = group_rows.shape[1]
    flat_rows = group_rows.reshape(-1)
    valid = flat_rows >= 0
    order_rank = jnp.cumsum(valid.astype(jnp.int32)) - 1
    pairs = jnp.sum(valid.astype(jnp.int32))
    turns = (pairs - position + 7) // 8

    def add_spread(step, totals):
        wanted = position + 8 * step
        slot = jnp.argmax(valid & (order_rank == wanted))
        target = slot // columns
        source = flat_rows[slot] - start_leaf
        return totals.at[target].add(nearby_block(target, source))

    totals = lax.fori_loop(0, turns, add_spread, jnp.zeros((8, leaf_size, width), jnp.float32))
    summed = lax.psum_scatter(
        totals.reshape(2, 4 * leaf_size, width), "grp", scatter_dimension=1, tiled=True
    )
    mine_part = jnp.where(parity == 0, summed[0], summed[1])
    other_part = jnp.where(parity == 0, summed[1], summed[0])
    near = mine_part + partner(other_part, "leaf", 0)
    total = near + distant_field
    return jnp.zeros_like(total).at[local].set(total)


def solution(mesh):
    return jax.shard_map(
        body,
        mesh=mesh,
        in_specs=(
            P(("leaf", "grp"), None),
            P(("leaf", "grp"), None),
            P(("leaf", "grp")),
            P(("leaf", "grp"), None),
            P(("leaf", "grp"), None),
            P(("leaf", "grp"), None),
            P(("leaf", "grp"), None),
            P(("leaf", "grp"), None),
            P(),
            P(),
        ),
        out_specs=P(("leaf", "grp"), None),
        check_vma=False,
    )
```

profile of v0, /device:TPU:0, one launch (start us, length us, event | category | flops | bytes accessed | tf_op | source)
XLA Modules:
  0.0 336.1 jit_solution(18068483424452420095)
XLA Ops:
  7.4 5.7 %gather_fusion = bf16[1024,256]{1,0:T(8,128)(2,1)} fusion(bf16[1024,256]{1,0:T(8,128)(2,1)} %param.14, s32[1024]{0:T(1024)S(1)} %get-tuple-element.172), kind=kCustom, calls=%fused_computation | custom fusion | bytes 1052672 | tf_op jit(solution)/shard_map/gather | solution.py:40
  13.2 4.0 %gather_fusion.1 = f32[1024,128]{1,0:T(8,128)} fusion(f32[1024,128]{1,0:T(8,128)S(1)} %copy-done.1, s32[1024]{0:T(1024)S(1)} %get-tuple-element.172), kind=kCustom, calls=%fused_computation.1 | custom fusion | bytes 1052672 | tf_op jit(solution)/shard_map/gather | solution.py:41
  17.2 21.3 %all-gather.5.cloned.1.call-done = bf16[4096,256]{1,0:T(8,128)(2,1)} async-done(((bf16[1024,256]{1,0:T(8,128)(2,1)}), bf16[4096,256]{1,0:T(8,128)(2,1)}) %all-gather.5.cloned.1.call-update) | async-done | bytes 2097168 | tf_op jit(solution)/shard_map/all_gather | solution.py:82
  38.6 1.5 collective-permute-start
  40.0 2.7 fusion.79
  42.7 20.0 %all-gather.7.cloned.1.call-done = f32[4096,128]{1,0:T(8,128)} async-done(((f32[1024,128]{1,0:T(8,128)}), f32[4096,128]{1,0:T(8,128)}) %all-gather.7.cloned.1.call-update) | async-done | bytes 2097168 | tf_op jit(solution)/shard_map/all_gather | solution.py:83
  62.7 1.5 collective-permute-start.1
  64.2 1.8 convolution_bitcast_fusion.1
  68.8 1.4 reduce-window.9
  70.9 1.8 convolution_bitcast_fusion.3
  73.6 30.3 %all-reduce.3.cloned.1.call-done = f32[256,128]{0,1:T(8,128)} async-done(((f32[256,128]{0,1:T(8,128)}), f32[256,128]{0,1:T(8,128)}) %all-reduce.3.cloned.1.call-update) | async-done | bytes 131088 | tf_op jit(solution)/shard_map/psum | solution.py:54
  103.9 1.8 convolution_bitcast_fusion.2
  105.8 4.2 %maximum_select_fusion = bf16[8192,256]{1,0:T(8,128)(2,1)} fusion(bf16[4096,256]{1,0:T(8,128)(2,1)} %collective-permute-done, bf16[4096,256]{1,0:T(8,128)(2,1)S(1)} %copy-done.2, pred[]{:T(512)S(6)} %eq.45), kind=kLoop, calls=%fused_computation.36 | loop fusion | flops 18874368 | bytes 8388609 | tf_op jit(solution)/shard_map/jit(_where)/select_n | solution.py:86
  110.1 21.5 %collective-permute-done.1 = f32[4096,128]{1,0:T(8,128)} collective-permute-done((f32[4096,128]{1,0:T(8,128)}, f32[4096,128]{1,0:T(8,128)}, u32[]{:S(2)}, u32[]{:S(2)}) %collective-permute-start.1) | collective-permute-done | bytes 2097184 | tf_op jit(solution)/shard_map/ppermute | solution.py:10
  131.6 4.7 %maximum_select_fusion.1 = f32[8192,128]{1,0:T(8,128)} fusion(f32[4096,128]{1,0:T(8,128)} %collective-permute-done.1, f32[4096,128]{1,0:T(8,128)S(1)} %copy-done.3, pred[]{:T(512)S(6)} %eq.45), kind=kLoop, calls=%fused_computation.37 | loop fusion | flops 3145728 | bytes 8388609 | tf_op jit(solution)/shard_map/jit(_where)/select_n | solution.py:91
  136.3 2.3 broadcast_in_dim.8
  138.6 47.8 %while.13 = (s32[]{:T(128)}, f32[8,1024,128]{2,1,0:T(8,128)}, s32[]{:T(128)}, s32[]{:T(128)}, s32[64]{0:T(128)S(1)}, /*index=5*/pred[64]{0:T(512)(128)(4,1)S(1)}...) while((s32[]{:T(128)}, f32[8,1024,128]{2,1,0:T(8,128)}, ...), condition=%wide.region_7.8_spmd, body=%wide.region_2.0_spmd.sunk | while | flops 2157705728 | bytes 12076940 | solution.py:117
  145.0 1.5 multiply_reduce_fusion.5
  146.6 1.9 fusion.105
  148.5 14.0 %fusion.106 = f32[8,1024,128]{2,1,0:T(8,128)} fusion(f32[8,1024,128]{2,1,0:T(8,128)} %get-tuple-element.264, s32[]{:T(128)} %select_n.197, f32[1024,1024]{1,0:T(8,128)S(1)} %fusion.105, f32[1024]{0:T(1024)S(1)} %get-tuple-element.240, f32[1024]{0:T(1024)S(1)} %get-tuple-element.241, f32[8192,128]{1,0:T(8,128)} %get-tuple-element.293, ...), kind=kOutput, calls=%fused_computation.22.clone.1 | convolution fusion | flops 1619263488 | bytes 5776388 | tf_op jit(solution)/shard_map/while/body/dot_general | solution.py:100
  168.9 1.6 multiply_reduce_fusion.5
  170.5 2.0 fusion.105
  172.5 13.9 %fusion.106 = f32[8,1024,128]{2,1,0:T(8,128)} fusion(f32[8,1024,128]{2,1,0:T(8,128)} %get-tuple-element.264, s32[]{:T(128)} %select_n.197, f32[1024,1024]{1,0:T(8,128)S(1)} %fusion.105, f32[1024]{0:T(1024)S(1)} %get-tuple-element.240, f32[1024]{0:T(1024)S(1)} %get-tuple-element.241, f32[8192,128]{1,0:T(8,128)} %get-tuple-element.293, ...), kind=kOutput, calls=%fused_computation.22.clone.1 | convolution fusion | flops 1619263488 | bytes 5776388 | tf_op jit(solution)/shard_map/while/body/dot_general | solution.py:100
  186.4 5.6 %copy.28 = f32[2,4096,128]{1,2,0:T(8,128)} copy(f32[2,4096,128]{2,1,0:T(8,128)} %bitcast.53) | data formatting | bytes 8388608 | tf_op jit(solution)/shard_map/reshape | solution.py:119
  192.7 57.3 %all_gather.17 = bf16[1024,256]{1,0:T(8,128)(2,1)S(1)} all-gather(bf16[32,256]{1,0:T(8,128)(2,1)S(1)} %copy-done.6), channel_id=1, replica_groups=mesh['leaf'=8,'grp'=4] {'leaf','grp'}, dimensions={0}, use_global_device_ids=true | all-gather | bytes 540672 | tf_op jit(solution)/shard_map/all_gather | solution.py:62
  251.6 5.7 %collective-permute-done.4 = f32[256,128]{0,1:T(8,128)S(1)} collective-permute-done((f32[256,128]{0,1:T(8,128)}, f32[256,128]{0,1:T(8,128)S(1)}, u32[]{:S(2)}, u32[]{:S(2)}) %collective-permute-start.4) | collective-permute-done | bytes 131104 | tf_op jit(solution)/shard_map/ppermute | solution.py:10
  258.3 40.2 %all_gather.18 = f32[1024,128]{1,0:T(8,128)S(1)} all-gather(f32[32,128]{1,0:T(8,128)S(1)} %copy.29), channel_id=1, replica_groups=mesh['leaf'=8,'grp'=4] {'leaf','grp'}, dimensions={0}, use_global_device_ids=true | all-gather | bytes 540672 | tf_op jit(solution)/shard_map/all_gather | solution.py:63
  298.5 3.0 fusion.37
  302.7 5.4 %all_gather.19 = f32[256,128]{1,0:T(8,128)S(1)} all-gather(f32[64,128]{1,0:T(8,128)S(1)} %convolution_bitcast_fusion.5), channel_id=1, replica_groups=mesh['leaf'=8,'grp'=4] {'grp'}, dimensions={0}, use_global_device_ids=true | all-gather | bytes 163840 | tf_op jit(solution)/shard_map/all_gather | solution.py:70
  311.4 12.2 %collective-permute-done.2 = f32[1024,128]{0,1:T(8,128)S(1)} collective-permute-done((f32[1024,128]{0,1:T(8,128)S(1)}, f32[1024,128]{0,1:T(8,128)S(1)}, u32[]{:S(2)}, u32[]{:S(2)}) %collective-permute-start.2) | collective-permute-done | bytes 524320 | tf_op jit(solution)/shard_map/ppermute | solution.py:10
  323.6 1.9 fusion.48
  325.7 3.9 %scatter_custom_fusion = f32[1024,128]{1,0:T(8,128)} fusion(s32[1024]{0:T(1024)S(1)} %get-tuple-element.173, f32[1024,128]{1,0:T(8,128)S(1)} %copy.30, f32[]{:T(128)} %constant.206.clone.1), kind=kCustom, calls=%fused_computation.65 | custom fusion | bytes 524292 | tf_op jit(solution)/shard_map/scatter | solution.py:125
  (68 shorter events, 16.5 us)
Async XLA Ops:
  6.5 33.5 %copy-start = (f32[256,1024]{1,0:T(8,128)S(1)}, f32[256,1024]{1,0:T(8,128)}, u32[]{:S(2)}) copy-start(f32[256,1024]{1,0:T(8,128)} %param.17) | copy-start | bytes 3145732
  6.5 6.6 %copy-start.1 = (f32[1024,128]{1,0:T(8,128)S(1)}, f32[1024,128]{1,0:T(8,128)}, u32[]{:S(2)}) copy-start(f32[1024,128]{1,0:T(8,128)} %param.15) | copy-start | bytes 1572868
  6.5 32.0 %all-gather.5.cloned.1.call-start = ((), (), s32[]{:S(2)}) async-start(), calls=%async_computation.4 | async-start | bytes 2621440 | tf_op jit(solution)/shard_map/all_gather | solution.py:82
  13.1 51.1 %copy-start.4 = (f32[256,256]{1,0:T(8,128)S(1)}, f32[256,256]{1,0:T(8,128)}, u32[]{:S(2)}) copy-start(f32[256,256]{1,0:T(8,128)} %param.18) | copy-start | bytes 786436
  13.1 52.9 %copy-start.8 = (s32[32,8]{0,1:T(8,128)S(1)}, s32[32,8]{0,1:T(8,128)}, u32[]{:S(2)}) copy-start(s32[32,8]{0,1:T(8,128)} %param.22) | copy-start | bytes 3076
  13.1 57.8 %copy-start.5 = (f32[128,256]{1,0:T(8,128)S(1)}, f32[128,256]{1,0:T(8,128)}, u32[]{:S(2)}) copy-start(f32[128,256]{1,0:T(8,128)} %param.19) | copy-start | bytes 393220
  13.1 49.6 %all-gather.7.cloned.1.call-start = ((), (), s32[]{:S(2)}) async-start(), calls=%async_computation.5 | async-start | bytes 2621440 | tf_op jit(solution)/shard_map/all_gather | solution.py:83
  17.2 86.7 %all-reduce.3.cloned.1.call-start = ((), (), s32[]{:S(2)}) async-start(), calls=%async_computation.2 | async-start | bytes 262144 | tf_op jit(solution)/shard_map/psum | solution.py:54
  38.6 67.3 %copy-start.2 = (bf16[4096,256]{1,0:T(8,128)(2,1)S(1)}, bf16[4096,256]{1,0:T(8,128)(2,1)}, u32[]{:S(2)}) copy-start(bf16[4096,256]{1,0:T(8,128)(2,1)} %all-gather.5.cloned.1.call-done) | copy-start | bytes 6291460
  38.6 67.3 %collective-permute-start = (bf16[4096,256]{1,0:T(8,128)(2,1)}, bf16[4096,256]{1,0:T(8,128)(2,1)}, u32[]{:S(2)}, u32[]{:S(2)}) collective-permute-start(bf16[4096,256]{1,0:T(8,128)(2,1)} %all-gather.5.cloned.1.call-done), channel_id=1, source_target_pairs={{0,4},{4,0},{8,12},{12,8},{16,20},{20,16},{24,28},{28,24},{1,5},{5... | collective-permute-start | bytes 6291464 | tf_op jit(solution)/shard_map/ppermute | solution.py:10
  62.7 68.9 %collective-permute-start.1 = (f32[4096,128]{1,0:T(8,128)}, f32[4096,128]{1,0:T(8,128)}, u32[]{:S(2)}, u32[]{:S(2)}) collective-permute-start(f32[4096,128]{1,0:T(8,128)} %all-gather.7.cloned.1.call-done), channel_id=1, source_target_pairs={{0,4},{4,0},{8,12},{12,8},{16,20},{20,16},{24,28},{28,24},{1,5},{5... | collective-permute-start | bytes 6291464 | tf_op jit(solution)/shard_map/ppermute | solution.py:10
  66.0 4.8 %collective-permute-start.3 = (f32[256,128]{0,1:T(8,128)}, f32[256,128]{0,1:T(8,128)}, u32[]{:S(2)}, u32[]{:S(2)}) collective-permute-start(f32[256,128]{0,1:T(8,128)} %convolution_bitcast_fusion.1), channel_id=1, source_target_pairs={{0,1},{1,0},{2,3},{3,2},{4,5},{5,4},{6,7},{7,6},{8,9},{9,8},{10,11... | collective-permute-start | bytes 393224 | tf_op jit(solution)/shard_map/ppermute | solution.py:10
  72.7 178.6 %all-reduce.5.cloned.1.call-start = ((), (), s32[]{:S(2)}) async-start(), calls=%async_computation.3 | async-start | bytes 262144 | tf_op jit(solution)/shard_map/psum | solution.py:58
  105.7 202.3 %reduce-scatter.2.cloned.1.call-start = ((), (), s32[]{:S(2)}) async-start(), calls=%async_computation.1 | async-start | bytes 5242880 | tf_op jit(solution)/shard_map/reduce_scatter | solution.py:118
  105.8 25.8 %copy-start.3 = (f32[4096,128]{1,0:T(8,128)S(1)}, f32[4096,128]{1,0:T(8,128)}, u32[]{:S(2)}) copy-start(f32[4096,128]{1,0:T(8,128)} %all-gather.7.cloned.1.call-done) | copy-start | bytes 6291460
  136.3 2.3 copy-start.7
  136.3 2.3 copy-start.9
  192.0 0.7 copy-start.6
  251.3 6.0 %collective-permute-start.4 = (f32[256,128]{0,1:T(8,128)}, f32[256,128]{0,1:T(8,128)S(1)}, u32[]{:S(2)}, u32[]{:S(2)}) collective-permute-start(f32[256,128]{0,1:T(8,128)} %all-reduce.5.cloned.1.call-done), channel_id=1, source_target_pairs={{0,4},{4,0},{8,12},{12,8},{16,20},{20,16},{24,28},{28,24},{1,5},{5... | collective-permute-start | bytes 393224 | tf_op jit(solution)/shard_map/ppermute | solution.py:10
  309.3 14.2 %collective-permute-start.2 = (f32[1024,128]{0,1:T(8,128)S(1)}, f32[1024,128]{0,1:T(8,128)S(1)}, u32[]{:S(2)}, u32[]{:S(2)}) collective-permute-start(f32[1024,128]{0,1:T(8,128)S(1)} %select_bitcast_fusion), channel_id=1, source_target_pairs={{0,4},{4,0},{8,12},{12,8},{16,20},{20,16},{24,28},{28,24},{1,5},{5... | collective-permute-start | bytes 1572872 | tf_op jit(solution)/shard_map/ppermute | solution.py:10
  309.7 1.3 collective-permute-start.5
Sparse Core Ops, SparseCore 0:
  13.2 25.2 all-gather.4
  40.1 22.5 all-gather.6
  72.8 31.0 all-reduce.2
  106.0 31.7 all-reduce.4
  192.2 67.5 reduce-scatter.1
where the time goes:
time: 337 us; the launch traced here: 336 us
  waiting for transfers between devices  112 us (33%)
  blocking collectives  103 us (31%)
  matrix products  47 us (14%)
  local copies, waits for them, and re-layouts  25.8 us (8%)
  other arithmetic  22 us (7%)
  between operations  14 us (4%)
  loops' own time  8.76 us (3%)
  starting transfers between devices  3.67 us (1%)
    all_gather x1, blocking collectives, body(): all_pts = lax.all_gather(skel_points, ('leaf', 'grp'), axis=0, tiled=True)  57.3 us
    ppermute x6, waiting for transfers between devices, partner(): return lax.ppermute(value, axis, pairs)  40.3 us
    all_gather x1, blocking collectives, body(): lax.all_gather(weight_rows, ('leaf', 'grp'), axis=0, tiled=True)  40.2 us
    psum x1, waiting for transfers between devices, body(): skel_two = lax.psum(part_two, 'grp')  30.3 us
    dot_general x2, matrix products, nearby_block(): return jnp.dot(kernel_block(left, right), source_w, precision=upper_limit)  27.9 us
    all_gather x1, waiting for transfers between devices, body(): four_pts = lax.all_gather(tree_pts, 'grp', axis=0, tiled=True)  21.3 us
    all_gather x1, waiting for transfers between devices, body(): four_w = lax.all_gather(tree_weight, 'grp', axis=0, tiled=True)  20 us
    another operation x1, loops' own time, body(): lax.fori_loop(0, turns, add_spread, jnp.zeros((8, leaf_size, width), jnp....  8.76 us
  transfers between devices with their start and end apart: 11, of which 7 were waited for; matrix products, arithmetic and copies ran while one was open for 24% of the time, Pallas kernels for 0%

commit v1 on v0

--- a/solution.py
+++ b/solution.py
@@ -51,7 +51,9 @@
     half = rank // 2
     rows_one = lax.dynamic_slice_in_dim(skel_one, flat % 2 * half, half, 0)
     part_two = jnp.dot(climb_pair.T, rows_one, precision=upper_limit)
-    skel_two = lax.psum(part_two, "grp")
+    skel_two = part_two
+    for hop in (1, 2):
+        skel_two = skel_two + lax.ppermute(skel_two, "grp", [(dev, dev ^ hop) for dev in range(4)])
     quarter = rank // 4
     rows_two = lax.dynamic_slice_in_dim(skel_two, grp_idx * quarter, quarter, 0)
     part_three = jnp.dot(climb_quad.T, rows_two, precision=upper_limit)

time: 337 us -> 340 us (level)
    psum x1 -> x0, waiting for transfers between devices: 30.3 us -> none  [body(): skel_two = lax.psum(part_two, 'grp')]
    ppermute x6, waiting for transfers between devices: 40.3 us -> 68.2 us  [partner(): return lax.ppermute(value, axis, pairs)]
  transfers between devices with their start and end apart: 11 -> 12, of which waited for: 7 -> 10; matrix products, arithmetic and copies ran while one was open for 24% -> 24% of each run, Pallas kernels for 0% -> 0%
where the time goes in v1:
time: 340 us; the launch traced here: 339 us
  waiting for transfers between devices  111 us (33%)
  blocking collectives  104 us (31%)
  matrix products  46.5 us (14%)
  local copies, waits for them, and re-layouts  25.9 us (8%)
  other arithmetic  23.6 us (7%)
  between operations  14 us (4%)
  loops' own time  9.64 us (3%)
  starting transfers between devices  4.41 us (1%)
    ppermute x6, waiting for transfers between devices, partner(): return lax.ppermute(value, axis, pairs)  68.2 us
    all_gather x1, blocking collectives, body(): all_pts = lax.all_gather(skel_points, ('leaf', 'grp'), axis=0, tiled=True)  58 us
    all_gather x1, blocking collectives, body(): lax.all_gather(weight_rows, ('leaf', 'grp'), axis=0, tiled=True)  40.1 us
    dot_general x2, matrix products, nearby_block(): return jnp.dot(kernel_block(left, right), source_w, precision=upper_limit)  28 us
    all_gather x1, waiting for transfers between devices, body(): four_pts = lax.all_gather(tree_pts, 'grp', axis=0, tiled=True)  21.3 us
    all_gather x1, waiting for transfers between devices, body(): four_w = lax.all_gather(tree_weight, 'grp', axis=0, tiled=True)  20 us
    another operation x1, loops' own time, body(): lax.fori_loop(0, turns, add_spread, jnp.zeros((8, leaf_size, width), jnp....  9.64 us
  transfers between devices with their start and end apart: 12, of which 10 were waited for; matrix products, arithmetic and copies ran while one was open for 24% of the time, Pallas kernels for 0%

profile of v1, /device:TPU:0, one launch (start us, length us, event | category | flops | bytes accessed | tf_op | source)
XLA Modules:
  0.0 338.5 jit_solution(14581231371489984871)
XLA Ops:
  6.5 1.4 broadcast_clamp_fusion
  8.0 5.7 %gather_fusion = bf16[1024,256]{1,0:T(8,128)(2,1)} fusion(bf16[1024,256]{1,0:T(8,128)(2,1)} %param.14, s32[1024]{0:T(1024)S(1)} %get-tuple-element.172), kind=kCustom, calls=%fused_computation | custom fusion | bytes 1052672 | tf_op jit(solution)/shard_map/gather | solution.py:40
  13.8 4.0 %gather_fusion.1 = f32[1024,128]{1,0:T(8,128)} fusion(f32[1024,128]{1,0:T(8,128)S(1)} %copy-done.1, s32[1024]{0:T(1024)S(1)} %get-tuple-element.172), kind=kCustom, calls=%fused_computation.1 | custom fusion | bytes 1052672 | tf_op jit(solution)/shard_map/gather | solution.py:41
  17.8 21.3 %all-gather.5.cloned.1.call-done = bf16[4096,256]{1,0:T(8,128)(2,1)} async-done(((bf16[1024,256]{1,0:T(8,128)(2,1)}), bf16[4096,256]{1,0:T(8,128)(2,1)}) %all-gather.5.cloned.1.call-update) | async-done | bytes 2097168 | tf_op jit(solution)/shard_map/all_gather | solution.py:84
  39.1 1.5 collective-permute-start
  40.6 2.7 fusion.79
  43.3 20.0 %all-gather.7.cloned.1.call-done = f32[4096,128]{1,0:T(8,128)} async-done(((f32[1024,128]{1,0:T(8,128)}), f32[4096,128]{1,0:T(8,128)}) %all-gather.7.cloned.1.call-update) | async-done | bytes 2097168 | tf_op jit(solution)/shard_map/all_gather | solution.py:85
  63.3 1.5 collective-permute-start.1
  64.8 1.8 convolution_bitcast_fusion.1
  74.2 1.4 reduce-window.9
  77.4 1.9 convolution_bitcast_fusion.2
  79.3 8.6 %collective-permute-done = bf16[4096,256]{1,0:T(8,128)(2,1)} collective-permute-done((bf16[4096,256]{1,0:T(8,128)(2,1)}, bf16[4096,256]{1,0:T(8,128)(2,1)}, u32[]{:S(2)}, u32[]{:S(2)}) %collective-permute-start) | collective-permute-done | bytes 2097184 | tf_op jit(solution)/shard_map/ppermute | solution.py:10
  88.0 4.2 %maximum_select_fusion = bf16[8192,256]{1,0:T(8,128)(2,1)} fusion(bf16[4096,256]{1,0:T(8,128)(2,1)} %collective-permute-done, bf16[4096,256]{1,0:T(8,128)(2,1)S(1)} %copy-done.2, pred[]{:T(512)S(6)} %eq.45), kind=kLoop, calls=%fused_computation.36 | loop fusion | flops 18874368 | bytes 8388609 | tf_op jit(solution)/shard_map/jit(_where)/select_n | solution.py:88
  92.2 40.0 %collective-permute-done.1 = f32[4096,128]{1,0:T(8,128)} collective-permute-done((f32[4096,128]{1,0:T(8,128)}, f32[4096,128]{1,0:T(8,128)}, u32[]{:S(2)}, u32[]{:S(2)}) %collective-permute-start.1) | collective-permute-done | bytes 2097184 | tf_op jit(solution)/shard_map/ppermute | solution.py:10
  132.2 4.7 %maximum_select_fusion.1 = f32[8192,128]{1,0:T(8,128)} fusion(f32[4096,128]{1,0:T(8,128)} %collective-permute-done.1, f32[4096,128]{1,0:T(8,128)S(1)} %copy-done.3, pred[]{:T(512)S(6)} %eq.45), kind=kLoop, calls=%fused_computation.37 | loop fusion | flops 3145728 | bytes 8388609 | tf_op jit(solution)/shard_map/jit(_where)/select_n | solution.py:93
  136.9 2.3 broadcast_in_dim.8
  139.2 48.9 %while.13 = (s32[]{:T(128)}, f32[8,1024,128]{2,1,0:T(8,128)}, s32[]{:T(128)}, s32[]{:T(128)}, s32[64]{0:T(128)S(1)}, /*index=5*/pred[64]{0:T(512)(128)(4,1)S(1)}...) while((s32[]{:T(128)}, f32[8,1024,128]{2,1,0:T(8,128)}, ...), condition=%wide.region_7.8_spmd, body=%wide.region_2.0_spmd.sunk | while | flops 2157705728 | bytes 12076940 | solution.py:119
  146.1 1.5 multiply_reduce_fusion.5
  147.7 1.9 fusion.105
  149.6 14.0 %fusion.106 = f32[8,1024,128]{2,1,0:T(8,128)} fusion(f32[8,1024,128]{2,1,0:T(8,128)} %get-tuple-element.265, s32[]{:T(128)} %select_n.197, f32[1024,1024]{1,0:T(8,128)S(1)} %fusion.105, f32[1024]{0:T(1024)S(1)} %get-tuple-element.241, f32[1024]{0:T(1024)S(1)} %get-tuple-element.242, f32[8192,128]{1,0:T(8,128)} %get-tuple-element.294, ...), kind=kOutput, calls=%fused_computation.22.clone.1 | convolution fusion | flops 1619263488 | bytes 5776388 | tf_op jit(solution)/shard_map/while/body/dot_general | solution.py:102
  170.6 1.6 multiply_reduce_fusion.5
  172.2 2.0 fusion.105
  174.1 14.0 %fusion.106 = f32[8,1024,128]{2,1,0:T(8,128)} fusion(f32[8,1024,128]{2,1,0:T(8,128)} %get-tuple-element.265, s32[]{:T(128)} %select_n.197, f32[1024,1024]{1,0:T(8,128)S(1)} %fusion.105, f32[1024]{0:T(1024)S(1)} %get-tuple-element.241, f32[1024]{0:T(1024)S(1)} %get-tuple-element.242, f32[8192,128]{1,0:T(8,128)} %get-tuple-element.294, ...), kind=kOutput, calls=%fused_computation.22.clone.1 | convolution fusion | flops 1619263488 | bytes 5776388 | tf_op jit(solution)/shard_map/while/body/dot_general | solution.py:102
  188.1 5.6 %copy.28 = f32[2,4096,128]{1,2,0:T(8,128)} copy(f32[2,4096,128]{2,1,0:T(8,128)} %bitcast.53) | data formatting | bytes 8388608 | tf_op jit(solution)/shard_map/reshape | solution.py:121
  194.5 58.0 %all_gather.17 = bf16[1024,256]{1,0:T(8,128)(2,1)S(1)} all-gather(bf16[32,256]{1,0:T(8,128)(2,1)S(1)} %copy-done.6), channel_id=1, replica_groups=mesh['leaf'=8,'grp'=4] {'leaf','grp'}, dimensions={0}, use_global_device_ids=true | all-gather | bytes 540672 | tf_op jit(solution)/shard_map/all_gather | solution.py:64
  254.0 5.7 %collective-permute-done.6 = f32[256,128]{0,1:T(8,128)S(1)} collective-permute-done((f32[256,128]{0,1:T(8,128)}, f32[256,128]{0,1:T(8,128)S(1)}, u32[]{:S(2)}, u32[]{:S(2)}) %collective-permute-start.6) | collective-permute-done | bytes 131104 | tf_op jit(solution)/shard_map/ppermute | solution.py:10
  260.7 40.1 %all_gather.18 = f32[1024,128]{1,0:T(8,128)S(1)} all-gather(f32[32,128]{1,0:T(8,128)S(1)} %copy.29), channel_id=1, replica_groups=mesh['leaf'=8,'grp'=4] {'leaf','grp'}, dimensions={0}, use_global_device_ids=true | all-gather | bytes 540672 | tf_op jit(solution)/shard_map/all_gather | solution.py:65
  300.9 3.0 fusion.37
  305.0 5.4 %all_gather.19 = f32[256,128]{1,0:T(8,128)S(1)} all-gather(f32[64,128]{1,0:T(8,128)S(1)} %convolution_bitcast_fusion.5), channel_id=1, replica_groups=mesh['leaf'=8,'grp'=4] {'grp'}, dimensions={0}, use_global_device_ids=true | all-gather | bytes 163840 | tf_op jit(solution)/shard_map/all_gather | solution.py:72
  313.7 12.2 %collective-permute-done.2 = f32[1024,128]{0,1:T(8,128)S(1)} collective-permute-done((f32[1024,128]{0,1:T(8,128)S(1)}, f32[1024,128]{0,1:T(8,128)S(1)}, u32[]{:S(2)}, u32[]{:S(2)}) %collective-permute-start.2) | collective-permute-done | bytes 524320 | tf_op jit(solution)/shard_map/ppermute | solution.py:10
  325.9 1.9 fusion.48
  328.0 4.0 %scatter_custom_fusion = f32[1024,128]{1,0:T(8,128)} fusion(s32[1024]{0:T(1024)} %get-tuple-element.173, f32[1024,128]{1,0:T(8,128)S(1)} %copy.30, f32[]{:T(128)} %constant.206.clone.1), kind=kCustom, calls=%fused_computation.65 | custom fusion | bytes 524800 | tf_op jit(solution)/shard_map/scatter | solution.py:127
  (69 shorter events, 20.9 us)
Async XLA Ops:
  6.5 34.1 %copy-start = (f32[256,1024]{1,0:T(8,128)S(1)}, f32[256,1024]{1,0:T(8,128)}, u32[]{:S(2)}) copy-start(f32[256,1024]{1,0:T(8,128)} %param.17) | copy-start | bytes 3145732
  6.5 7.2 %copy-start.1 = (f32[1024,128]{1,0:T(8,128)S(1)}, f32[1024,128]{1,0:T(8,128)}, u32[]{:S(2)}) copy-start(f32[1024,128]{1,0:T(8,128)} %param.15) | copy-start | bytes 1572868
  6.5 32.6 %all-gather.5.cloned.1.call-start = ((), (), s32[]{:S(2)}) async-start(), calls=%async_computation.3 | async-start | bytes 2621440 | tf_op jit(solution)/shard_map/all_gather | solution.py:84
  13.7 51.1 %copy-start.4 = (f32[256,256]{1,0:T(8,128)S(1)}, f32[256,256]{1,0:T(8,128)}, u32[]{:S(2)}) copy-start(f32[256,256]{1,0:T(8,128)} %param.18) | copy-start | bytes 786436
  13.7 52.9 %copy-start.8 = (s32[32,8]{0,1:T(8,128)S(1)}, s32[32,8]{0,1:T(8,128)}, u32[]{:S(2)}) copy-start(s32[32,8]{0,1:T(8,128)} %param.22) | copy-start | bytes 3076
  13.7 54.6 %copy-start.5 = (f32[128,256]{1,0:T(8,128)S(1)}, f32[128,256]{1,0:T(8,128)}, u32[]{:S(2)}) copy-start(f32[128,256]{1,0:T(8,128)} %param.19) | copy-start | bytes 393220
  13.7 49.6 %all-gather.7.cloned.1.call-start = ((), (), s32[]{:S(2)}) async-start(), calls=%async_computation.4 | async-start | bytes 2621440 | tf_op jit(solution)/shard_map/all_gather | solution.py:85
  17.8 235.9 %all-reduce.2.cloned.1.call-start = ((), (), s32[]{:S(2)}) async-start(), calls=%async_computation.2 | async-start | bytes 262144 | tf_op jit(solution)/shard_map/psum | solution.py:60
  39.1 48.8 %copy-start.2 = (bf16[4096,256]{1,0:T(8,128)(2,1)S(1)}, bf16[4096,256]{1,0:T(8,128)(2,1)}, u32[]{:S(2)}) copy-start(bf16[4096,256]{1,0:T(8,128)(2,1)} %all-gather.5.cloned.1.call-done) | copy-start | bytes 6291460
  39.1 48.8 %collective-permute-start = (bf16[4096,256]{1,0:T(8,128)(2,1)}, bf16[4096,256]{1,0:T(8,128)(2,1)}, u32[]{:S(2)}, u32[]{:S(2)}) collective-permute-start(bf16[4096,256]{1,0:T(8,128)(2,1)} %all-gather.5.cloned.1.call-done), channel_id=1, source_target_pairs={{0,4},{4,0},{8,12},{12,8},{16,20},{20,16},{24,28},{28,24},{1,5},{5... | collective-permute-start | bytes 6291464 | tf_op jit(solution)/shard_map/ppermute | solution.py:10
  63.3 68.9 %collective-permute-start.1 = (f32[4096,128]{1,0:T(8,128)}, f32[4096,128]{1,0:T(8,128)}, u32[]{:S(2)}, u32[]{:S(2)}) collective-permute-start(f32[4096,128]{1,0:T(8,128)} %all-gather.7.cloned.1.call-done), channel_id=1, source_target_pairs={{0,4},{4,0},{8,12},{12,8},{16,20},{20,16},{24,28},{28,24},{1,5},{5... | collective-permute-start | bytes 6291464 | tf_op jit(solution)/shard_map/ppermute | solution.py:10
  66.6 1.7 collective-permute-start.3
  69.4 1.4 collective-permute-start.4
  71.5 5.9 %collective-permute-start.5 = (f32[256,128]{0,1:T(8,128)}, f32[256,128]{0,1:T(8,128)}, u32[]{:S(2)}, u32[]{:S(2)}) collective-permute-start(f32[256,128]{0,1:T(8,128)} %add.151), channel_id=1, source_target_pairs={{0,2},{1,3},{2,0},{3,1},{4,6},{5,7},{6,4},{7,5},{8,10},{9,11},{10,... | collective-permute-start | bytes 393224 | tf_op jit(solution)/shard_map/ppermute | solution.py:56
  79.3 231.1 %reduce-scatter.2.cloned.1.call-start = ((), (), s32[]{:S(2)}) async-start(), calls=%async_computation.1 | async-start | bytes 5242880 | tf_op jit(solution)/shard_map/reduce_scatter | solution.py:120
  79.3 52.8 %copy-start.3 = (f32[4096,128]{1,0:T(8,128)S(1)}, f32[4096,128]{1,0:T(8,128)}, u32[]{:S(2)}) copy-start(f32[4096,128]{1,0:T(8,128)} %all-gather.7.cloned.1.call-done) | copy-start | bytes 6291460
  136.9 2.3 copy-start.7
  136.9 2.3 copy-start.9
  193.7 0.7 copy-start.6
  253.7 6.0 %collective-permute-start.6 = (f32[256,128]{0,1:T(8,128)}, f32[256,128]{0,1:T(8,128)S(1)}, u32[]{:S(2)}, u32[]{:S(2)}) collective-permute-start(f32[256,128]{0,1:T(8,128)} %all-reduce.2.cloned.1.call-done), channel_id=1, source_target_pairs={{0,4},{4,0},{8,12},{12,8},{16,20},{20,16},{24,28},{28,24},{1,5},{5... | collective-permute-start | bytes 393224 | tf_op jit(solution)/shard_map/ppermute | solution.py:10
  311.6 14.2 %collective-permute-start.2 = (f32[1024,128]{0,1:T(8,128)S(1)}, f32[1024,128]{0,1:T(8,128)S(1)}, u32[]{:S(2)}, u32[]{:S(2)}) collective-permute-start(f32[1024,128]{0,1:T(8,128)S(1)} %select_bitcast_fusion), channel_id=1, source_target_pairs={{0,4},{4,0},{8,12},{12,8},{16,20},{20,16},{24,28},{28,24},{1,5},{5... | collective-permute-start | bytes 1572872 | tf_op jit(solution)/shard_map/ppermute | solution.py:10
  312.0 1.3 collective-permute-start.7
Sparse Core Ops, SparseCore 0:
  13.8 25.2 all-gather.4
  40.7 22.5 all-gather.6
  79.4 30.8 all-reduce.1
  193.9 68.1 reduce-scatter.1
